TPU v7x, 16 devices: a 4x2x1 block of a 4x4x8 slice. The times are simulated.
16 devices in a mesh: dp: 4 (over y, z, core), tp: 4 (over x).
Axes of the slice: x: 4, y: 2, z: 1, core: 2. Of those that a mesh axis runs over, the one named last changes fastest.
The devices are a block of a 4x4x8 slice.
Arguments:
- x: bfloat16 [8192, 6656], P('dp'), parts along dimension 0
- w_gate: bfloat16 [6656, 17920], P(None, 'tp')
- w_up: bfloat16 [6656, 17920], P(None, 'tp')
- w_down: bfloat16 [17920, 6656], P('tp')
Outputs:
- output: bfloat16 [8192, 6656], P('dp'), parts along dimension 0
There are 4 independent parts. A program takes and returns all parts, laid end to end along the dimension named above; an argument that names none is the same for every part.
All inputs are finite; a program needn't handle non-finite values.
Results may differ from a plain program's by a relative error of at most 0.016.
Values are sent between devices in bfloat16 or wider.
A program may use at most 768 MiB of HBM per device.

v0:
```python
import jax
import jax.numpy as jnp
from jax import lax
from jax.sharding import PartitionSpec as P


def solution(mesh):
    def step(x, w_gate, w_up, w_down):
        gate = jnp.dot(x, w_gate, preferred_element_type=jnp.float32)
        up = jnp.dot(x, w_up, preferred_element_type=jnp.float32)
        hidden = (jax.nn.silu(gate) * up).astype(jnp.bfloat16)
        term = jnp.dot(hidden, w_down, preferred_element_type=jnp.float32).astype(jnp.bfloat16)
        return lax.psum(term, "tp")

    return jax.shard_map(
        step,
        mesh=mesh,
        in_specs=(P("dp", None), P(None, "tp"), P(None, "tp"), P("tp", None)),
        out_specs=P("dp", None),
        check_vma=False,
    )
```

profile of v0, /device:TPU:112, one launch (start us, length us, event | category | flops | bytes accessed | tf_op | source)
XLA Modules:
  0.0 922.2 jit_solution(4629467509290231558)
XLA Ops:
  6.5 0.0 all-reduce.2.cloned.1.call-start
  6.6 138.1 %fusion = f32[2048,4480]{1,0:T(8,128)} fusion(bf16[2048,6656]{1,0:T(8,128)(2,1)} %param.4, bf16[6656,4480]{1,0:T(8,128)(2,1)} %param.5), kind=kOutput, calls=%fused_computation.2 | convolution fusion | flops 122138132480 | bytes 123600896 | tf_op jit(solution)/shard_map/dot_general | solution.py:9
  144.7 153.8 %multiply_convert_fusion = bf16[2048,4480]{1,0:T(8,128)(2,1)} fusion(f32[2048,4480]{1,0:T(8,128)} %fusion, bf16[2048,6656]{1,0:T(8,128)(2,1)} %param.4, bf16[6656,4480]{1,0:T(8,128)(2,1)} %param.6), kind=kOutput, calls=%fused_computation | convolution fusion | flops 122193182720 | bytes 141950976 | tf_op jit(solution)/shard_map/dot_general | solution.py:10
  298.4 138.9 %convolution_convert_fusion = bf16[2048,6656]{1,0:T(8,128)(2,1)} fusion(bf16[2048,4480]{1,0:T(8,128)(2,1)} %multiply_convert_fusion, bf16[4480,6656]{1,0:T(8,128)(2,1)} %param.7), kind=kOutput, calls=%fused_computation.1 | convolution fusion | flops 122151763968 | bytes 105250816 | tf_op jit(solution)/shard_map/dot_general | solution.py:12
  437.4 0.1 all-reduce.2.cloned.1.call-update
  437.4 458.6 %all-reduce.2.cloned.1.call-done = bf16[2048,6656]{1,0:T(8,128)(2,1)} async-done(((bf16[2048,6656]{1,0:T(8,128)(2,1)}), bf16[2048,6656]{1,0:T(8,128)(2,1)}) %all-reduce.2.cloned.1.call-update) | async-done | bytes 27262992 | tf_op jit(solution)/shard_map/psum | solution.py:13
  896.0 19.3 %copy.6 = bf16[2048,6656]{1,0:T(8,128)(2,1)} copy(bf16[2048,6656]{1,0:T(8,128)(2,1)} %all-reduce.2.cloned.1.call-done) | data formatting | bytes 54525952
Async XLA Ops:
  6.5 889.5 %all-reduce.2.cloned.1.call-start = ((), (), s32[]{:S(2)}) async-start(), calls=%async_computation | async-start | bytes 54525952 | tf_op jit(solution)/shard_map/psum | solution.py:13
Sparse Core Ops, SparseCore 0:
  437.6 458.4 all-reduce.1
where the time goes:
time: 922 us
  waiting for transfers between devices  459 us (50%)
  matrix products  431 us (47%)
  local copies, waits for them, and re-layouts  19.3 us (2%)
  between operations  13.4 us (1%)
    psum x1, waiting for transfers between devices, step(): return lax.psum(term, 'tp')  459 us
    dot_general x1, matrix products, step(): up = jnp.dot(x, w_up, preferred_element_type=jnp.float32)  154 us
    dot_general x1, matrix products, step(): jnp.dot(hidden, w_down, preferred_element_type=jnp.float32)  139 us
    dot_general x1, matrix products, step(): gate = jnp.dot(x, w_gate, preferred_element_type=jnp.float32)  138 us
    unnamed x1, local copies, waits for them, and re-layouts  19.3 us
  transfers between devices with their start and end apart: 1, of which 1 were waited for; matrix products, arithmetic and copies ran while one was open for 0% of the time, Pallas kernels for 0%

commit v1 on v0

v1 whole, which is shorter than its diff:
```python
import functools

import jax
import jax.numpy as jnp
from jax import lax
from jax.experimental import pallas as pl
from jax.experimental.pallas import tpu as pltpu
from jax.sharding import PartitionSpec as P

MESH = pl.DeviceIdType.MESH
LANES = 128
PARTS = (5, 6, 7, 8, 6)
SLOTS = 18
WBUF = 3


def kernel(n, sizes, x_ref, wg_ref, wu_ref, wd_ref, y_ref,
           xv, wv, hid, own, s0, s1, fin, rv, xsem, wsem, ssem, rsem, lsem):
    me = lax.axis_index("tp")
    right, left, far = lax.rem(me + 1, n), lax.rem(me + n - 1, n), lax.rem(me + 2, n)
    d, f = wg_ref.shape
    share = d // n
    units = share // LANES
    wide = 2 * LANES
    full, tail = f // wide, f % wide
    tiles = full + (1 if tail else 0)
    steps = tiles + units
    starts = [sum(sizes[:k]) for k in range(len(sizes))]
    last = len(sizes) - 1

    barrier = pltpu.get_barrier_semaphore()
    for nb in (left, right):
        pl.semaphore_signal(barrier, inc=1, device_id={"tp": nb}, device_id_type=MESH)
    pl.semaphore_wait(barrier, 2)

    def wslot(k, q):
        return lax.rem(k * steps + q, WBUF)

    def load_gu(k, i, width):
        b = wslot(k, i)
        c = pl.ds(pl.multiple_of(i * wide, LANES), width)
        return [
            pltpu.make_async_copy(wg_ref.at[:, c], wv.at[b, :, pl.ds(0, width)], wsem.at[b, 0]),
            pltpu.make_async_copy(wu_ref.at[:, c], wv.at[b, :, pl.ds(width, width)], wsem.at[b, 1]),
        ]

    def load_d(k, u):
        b = wslot(k, tiles + u)
        out = []
        for j in range(n):
            owner = lax.rem(me + 1 + j, n)
            c = pl.ds(pl.multiple_of(owner * share + u * LANES, LANES), LANES)
            out.append(pltpu.make_async_copy(
                wd_ref.at[:, c], wv.at[b, pl.ds(0, f), pl.ds(j * LANES, LANES)], wsem.at[b, j]))
        return out

    def start(copies):
        for c in copies:
            c.start()

    def wait(copies):
        for c in copies:
            c.wait()

    def prefetch(k, q):
        if isinstance(q, int):
            if q >= steps:
                if k < last:
                    prefetch(k + 1, q - steps)
            elif q < full:
                start(load_gu(k, q, wide))
            elif q < tiles:
                start(load_gu(k, q, tail))
            else:
                start(load_d(k, q - tiles))
            return

        @pl.when(q < full)
        def _():
            start(load_gu(k, q, wide))

        if tail:
            @pl.when(q == full)
            def _():
                start(load_gu(k, full, tail))

        @pl.when(jnp.logical_and(q >= tiles, q < steps))
        def _():
            start(load_d(k, q - tiles))

        if k < last:
            @pl.when(q >= steps)
            def _():
                start(load_gu(k + 1, q - steps, wide))

    def load_x(k):
        m = sizes[k]
        return pltpu.make_async_copy(x_ref.at[pl.ds(starts[k], m)], xv.at[pl.ds(0, m)], xsem)

    def slot(k, u):
        return lax.rem(k * units + u, SLOTS)

    def cols(owner, u):
        return pl.ds(pl.multiple_of(owner * share + u * LANES, LANES), LANES)

    def remote(src, dst, s, send, recv, to):
        return pltpu.make_async_remote_copy(
            src, dst, ssem.at[send, s], rsem.at[recv, s], device_id={"tp": to}, device_id_type=MESH)

    def first_sends(k, u, js=(0, 1, 2, 3)):
        s, h = slot(k, u), sizes[k] // 2
        r = pl.ds(0, h)
        to = (right, left, left, right)
        return [remote(s0.at[s, j, r], rv.at[j, s, r], s, j, j, to[j]) for j in js]

    def second_sends(k, u):
        s, h = slot(k, u), sizes[k] // 2
        r = pl.ds(0, h)
        return [remote(s1.at[s, j, r], rv.at[4 + j, s, r], s, 4 + j, 4 + j, to)
                for j, to in enumerate((right, left))]

    def rows(k, half=None):
        m = sizes[k]
        if half is None:
            return pl.ds(starts[k], m)
        return pl.ds(starts[k] + half * (m // 2), m // 2)

    def result_sends(k, u, owners):
        s = slot(k, u)
        return [remote(fin.at[s, pl.ds(0, sizes[k])], y_ref.at[rows(k), cols(o, u)], s, 6 + j, 6 + j, to)
                for j, (o, to) in enumerate(zip(owners, (right, left)))]

    def result_local(k, u):
        s = slot(k, u)
        return pltpu.make_async_copy(
            fin.at[s, pl.ds(0, sizes[k])], y_ref.at[rows(k), cols(me, u)], lsem.at[s])

    def relays(k, u, owners):
        s = slot(k, u)
        out = []
        for j, (o, to) in enumerate(zip(owners, (right, left))):
            piece = y_ref.at[rows(k, j), cols(o, u)]
            out.append(remote(piece, piece, s, 8 + j, 8 + j, to))
        return out

    def unit(k, u):
        m = sizes[k]
        h = m // 2
        s = slot(k, u)
        b = wslot(k, tiles + u)
        acc = jnp.dot(hid[pl.ds(0, m)], wv[b, pl.ds(0, f)], preferred_element_type=jnp.float32)
        top, low = acc[:h], acc[h:]

        def part(a, j):
            return a[:, j * LANES:(j + 1) * LANES]

        r = pl.ds(0, h)
        s0[s, 0, r] = part(top, 1).astype(jnp.bfloat16)
        s0[s, 1, r] = part(low, 1).astype(jnp.bfloat16)
        s0[s, 2, r] = part(top, 2).astype(jnp.bfloat16)
        s0[s, 3, r] = part(low, 0).astype(jnp.bfloat16)
        own[s, 0, r] = part(top, 0)
        own[s, 1, r] = part(low, 2)
        own[s, 2, r] = part(top, 3)
        own[s, 3, r] = part(low, 3)
        start(first_sends(k, u))

    def stage1(k, u):
        s, h = slot(k, u), sizes[k] // 2
        r = pl.ds(0, h)
        arrived = first_sends(k, u, (0, 1))
        nxt = second_sends(k, u)
        for j in range(2):
            arrived[j].wait_recv()
            s1[s, j, r] = (rv[j, s, r].astype(jnp.float32) + own[s, j, r]).astype(jnp.bfloat16)
            nxt[j].start()

    def stage2(k, u):
        s, h = slot(k, u), sizes[k] // 2
        r = pl.ds(0, h)
        arrived = first_sends(k, u, (2, 3))
        summed = second_sends(k, u)
        for j in range(2):
            arrived[j].wait_recv()
            summed[j].wait_recv()
            v = rv[4 + j, s, r].astype(jnp.float32) + rv[2 + j, s, r].astype(jnp.float32)
            fin[s, pl.ds(j * h, h)] = (v + own[s, 2 + j, r]).astype(jnp.bfloat16)
        start(result_sends(k, u, (me, me)))
        result_local(k, u).start()
        for c in first_sends(k, u):
            c.wait_send()

    def stage3(k, u):
        arrived = result_sends(k, u, (left, right))
        out = relays(k, u, (left, right))
        for j in range(2):
            arrived[j].wait_recv()
            out[j].start()
        for c in second_sends(k, u):
            c.wait_send()

    def stage4(k, u):
        for c in relays(k, u, (far, far)):
            c.wait_recv()
        for c in result_sends(k, u, (me, me)):
            c.wait_send()
        result_local(k, u).wait()
        for c in relays(k, u, (left, right)):
            c.wait_send()

    def ticks(k, q, plan):
        for stage, (a, span) in zip((stage4, stage3, stage2, stage1), plan[::-1]):
            u = ((q - a) * units) // span if isinstance(q, int) else lax.div(
                jnp.maximum(q - a, 0) * units, span)
            v = ((q + 1 - a) * units) // span if isinstance(q, int) else lax.div(
                jnp.maximum(q + 1 - a, 0) * units, span)
            if isinstance(q, int):
                u, v = max(u, 0), max(v, 0)
                if q >= a and v > u and u < units:
                    stage(k, u)
            else:
                @pl.when(jnp.logical_and(jnp.logical_and(q >= a, v > u), u < units))
                def _():
                    stage(k, u)

    span = max(units, tiles - 3)
    plan = [(0, span), (2, span + 1), (4, span + 2), (6, span + 3)]
    plan_end = [(0, units), (2, units), (4, units), (6, units)]

    load_x(0).start()
    prefetch(0, 0)
    prefetch(0, 1)
    for k, m in enumerate(sizes):
        load_x(k).wait()

        def tile(i, width, k=k, m=m):
            b = wslot(k, i)
            wait(load_gu(k, i, width))
            acc = jnp.dot(xv[pl.ds(0, m)], wv[b, :, pl.ds(0, 2 * width)], preferred_element_type=jnp.float32)
            gate, up = acc[:, :width], acc[:, width:]
            c = pl.ds(pl.multiple_of(i * wide, LANES), width)
            hid[pl.ds(0, m), c] = (jax.nn.silu(gate) * up).astype(jnp.bfloat16)

        @pl.loop(0, full)
        def _(i, k=k):
            prefetch(k, i + 2)
            if k:
                ticks(k - 1, i, plan)
            tile(i, wide)

        if tail:
            prefetch(k, full + 2)
            if k:
                ticks(k - 1, full, plan)
            tile(full, tail)

        if k < last:
            load_x(k + 1).start()

        @pl.loop(0, units)
        def _(u, k=k):
            prefetch(k, tiles + u + 2)
            if k:
                ticks(k - 1, tiles + u, plan)
            wait(load_d(k, u))
            unit(k, u)

    @pl.loop(0, units + 6)
    def _(q):
        ticks(last, q, plan_end)


def solution(mesh):
    n = mesh.shape["tp"]

    def step(x, w_gate, w_up, w_down):
        t, d = x.shape
        f = w_gate.shape[1]
        sizes = [t * p // sum(PARTS) for p in PARTS]
        top = max(sizes)
        half = top // 2
        hbm = [pltpu.with_memory_space_constraint(a, pltpu.HBM) for a in (x, w_gate, w_up, w_down)]
        bf = jnp.bfloat16
        return pl.pallas_call(
            functools.partial(kernel, n, sizes),
            out_shape=jax.ShapeDtypeStruct((t, d), bf),
            in_specs=[pl.BlockSpec(memory_space=pltpu.HBM)] * 4,
            out_specs=pl.BlockSpec(memory_space=pltpu.HBM),
            scratch_shapes=[
                pltpu.VMEM((top, d), bf),
                pltpu.VMEM((WBUF, max(d, f), 4 * LANES), bf),
                pltpu.VMEM((top, f), bf),
                pltpu.VMEM((SLOTS, 4, half, LANES), jnp.float32),
                pltpu.VMEM((SLOTS, 4, half, LANES), bf),
                pltpu.VMEM((SLOTS, 2, half, LANES), bf),
                pltpu.VMEM((SLOTS, top, LANES), bf),
                pltpu.VMEM((6, SLOTS, half, LANES), bf),
                pltpu.SemaphoreType.DMA,
                pltpu.SemaphoreType.DMA((WBUF, 4)),
                pltpu.SemaphoreType.DMA((10, SLOTS)),
                pltpu.SemaphoreType.DMA((10, SLOTS)),
                pltpu.SemaphoreType.DMA((SLOTS,)),
            ],
            name="mlp",
            compiler_params=pltpu.CompilerParams(
                collective_id=0, has_side_effects=True, vmem_limit_bytes=67043328),
            cost_estimate=pl.CostEstimate(flops=6 * t * d * f, bytes_accessed=6 * d * f, transcendentals=t * f),
        )(*hbm)

    return jax.shard_map(
        step,
        mesh=mesh,
        in_specs=(P("dp", None), P(None, "tp"), P(None, "tp"), P("tp", None)),
        out_specs=P("dp", None),
        check_vma=False,
    )
```

time: 922 us -> 543 us (0.59)
  Pallas kernels: 0 us -> 524 us
  waiting for transfers between devices: 459 us -> 0 us
  matrix products: 431 us -> 0 us
  between operations: 13.4 us -> 0.01 us
    pallas_call x0 -> x1, Pallas kernels: none -> 524 us  [step(): pl.pallas_call(functools.partial(kernel, n, sizes), out_shape=jax.ShapeDt...]
    psum x1 -> x0, waiting for transfers between devices: 459 us -> none  [step(): return lax.psum(term, 'tp')]
    dot_general x3 -> x0, matrix products: 431 us -> none  [the longest x1 154 us: step(): up = jnp.dot(x, w_up, preferred_element_type=jnp.float32)]
  transfers between devices with their start and end apart: 1 -> 0, of which waited for: 1 -> 0; matrix products, arithmetic and copies ran while one was open for 0% -> 0% of each run, Pallas kernels for 0% -> 0%
where the time goes in v1:
time: 543 us
  Pallas kernels  524 us (97%)
  local copies, waits for them, and re-layouts  19.3 us (4%)
    pallas_call x1, Pallas kernels, step(): pl.pallas_call(functools.partial(kernel, n, sizes), out_shape=jax.ShapeDt...  524 us
    unnamed x1, local copies, waits for them, and re-layouts  19.3 us

profile of v1, /device:TPU:112, one launch (start us, length us, event | category | flops | bytes accessed | tf_op | source)
XLA Modules:
  0.0 543.3 jit_solution(5461539107659455974)
XLA Ops:
  0.0 523.9 %mlp.1 = bf16[2048,6656]{1,0:T(8,128)(2,1)} custom-call(bf16[2048,6656]{1,0:T(8,128)(2,1)} %x_ref.1, bf16[6656,4480]{1,0:T(8,128)(2,1)} %wg_ref.1, bf16[6656,4480]{1,0:T(8,128)(2,1)} %wu_ref.1, bf16[4480,6656]{1,0:T(8,128)(2,1)} %wd_ref.1), custom_call_target="tpu_custom_call" | custom-call | flops 366414397440 | bytes 178913280 | tf_op jit(solution)/shard_map/mlp/pallas_call | solution.py:284
  523.9 19.3 %copy.6 = bf16[2048,6656]{1,0:T(8,128)(2,1)} copy(bf16[2048,6656]{1,0:T(8,128)(2,1)} %mlp.1) | data formatting | bytes 54525952

commit v2 on v1

--- a/solution.py
+++ b/solution.py
@@ -9,12 +9,16 @@
 
 MESH = pl.DeviceIdType.MESH
 LANES = 128
-PARTS = (5, 6, 7, 8, 6)
-SLOTS = 18
+PARTS = (11, 11, 11, 11, 11, 9)
+HELD = 4
+PLAN = ((0, 13), (3, 14), (6, 18), (11, 19))
+LAST = ((4, 13), (8, 13), (15, 13), (19, 20))
+SLOTS = 16
 WBUF = 3
-
-
-def kernel(n, sizes, x_ref, wg_ref, wu_ref, wd_ref, y_ref,
+VMEM = 66 * 10**6
+
+
+def kernel(n, sizes, x_ref, wg_ref, wu_ref, wd_ref, y_ref, yv_ref,
            xv, wv, hid, own, s0, s1, fin, rv, xsem, wsem, ssem, rsem, lsem):
     me = lax.axis_index("tp")
     right, left, far = lax.rem(me + 1, n), lax.rem(me + n - 1, n), lax.rem(me + 2, n)
@@ -27,11 +31,10 @@
     steps = tiles + units
     starts = [sum(sizes[:k]) for k in range(len(sizes))]
     last = len(sizes) - 1
-
-    barrier = pltpu.get_barrier_semaphore()
-    for nb in (left, right):
-        pl.semaphore_signal(barrier, inc=1, device_id={"tp": nb}, device_id_type=MESH)
-    pl.semaphore_wait(barrier, 2)
+    held = len(sizes) - HELD
+
+    plan = [(a, b * units // 13) for a, b in PLAN]
+    end = [(a, b * units // 13) for a, b in LAST]
 
     def wslot(k, q):
         return lax.rem(k * steps + q, WBUF)
@@ -62,7 +65,7 @@
         for c in copies:
             c.wait()
 
-    def prefetch(k, q):
+    def prefetch(k, q, first=0):
         if isinstance(q, int):
             if q >= steps:
                 if k < last:
@@ -75,11 +78,12 @@
                 start(load_d(k, q - tiles))
             return
 
-        @pl.when(q < full)
-        def _():
-            start(load_gu(k, q, wide))
-
-        if tail:
+        if not first:
+            @pl.when(q < full)
+            def _():
+                start(load_gu(k, q, wide))
+
+        if tail and not first:
             @pl.when(q == full)
             def _():
                 start(load_gu(k, full, tail))
@@ -88,7 +92,7 @@
         def _():
             start(load_d(k, q - tiles))
 
-        if k < last:
+        if first and k < last:
             @pl.when(q >= steps)
             def _():
                 start(load_gu(k + 1, q - steps, wide))
@@ -119,28 +123,31 @@
         return [remote(s1.at[s, j, r], rv.at[4 + j, s, r], s, 4 + j, 4 + j, to)
                 for j, to in enumerate((right, left))]
 
-    def rows(k, half=None):
+    def piece(k, owner, u, half=None):
         m = sizes[k]
-        if half is None:
-            return pl.ds(starts[k], m)
-        return pl.ds(starts[k] + half * (m // 2), m // 2)
+        ref, at = (y_ref, starts[k]) if k < held else (yv_ref, starts[k] - starts[held])
+        r = pl.ds(at, m) if half is None else pl.ds(at + half * (m // 2), m // 2)
+        return ref.at[r, cols(owner, u)]
 
     def result_sends(k, u, owners):
         s = slot(k, u)
-        return [remote(fin.at[s, pl.ds(0, sizes[k])], y_ref.at[rows(k), cols(o, u)], s, 6 + j, 6 + j, to)
-                for j, (o, to) in enumerate(zip(owners, (right, left)))]
+        out = []
+        for j, (o, to) in enumerate(zip(owners, (right, left))):
+            dst = piece(k, o, u)
+            src = fin.at[s, pl.ds(0, sizes[k])] if k < held else dst
+            out.append(remote(src, dst, s, 6 + j, 6 + j, to))
+        return out
 
     def result_local(k, u):
         s = slot(k, u)
-        return pltpu.make_async_copy(
-            fin.at[s, pl.ds(0, sizes[k])], y_ref.at[rows(k), cols(me, u)], lsem.at[s])
+        return pltpu.make_async_copy(fin.at[s, pl.ds(0, sizes[k])], piece(k, me, u), lsem.at[s])
 
     def relays(k, u, owners):
         s = slot(k, u)
         out = []
         for j, (o, to) in enumerate(zip(owners, (right, left))):
-            piece = y_ref.at[rows(k, j), cols(o, u)]
-            out.append(remote(piece, piece, s, 8 + j, 8 + j, to))
+            p = piece(k, o, u, j)
+            out.append(remote(p, p, s, 8 + j, 8 + j, to))
         return out
 
     def unit(k, u):
@@ -184,9 +191,14 @@
             arrived[j].wait_recv()
             summed[j].wait_recv()
             v = rv[4 + j, s, r].astype(jnp.float32) + rv[2 + j, s, r].astype(jnp.float32)
-            fin[s, pl.ds(j * h, h)] = (v + own[s, 2 + j, r]).astype(jnp.bfloat16)
+            v = (v + own[s, 2 + j, r]).astype(jnp.bfloat16)
+            if k < held:
+                fin[s, pl.ds(j * h, h)] = v
+            else:
+                yv_ref[pl.ds(starts[k] - starts[held] + j * h, h), cols(me, u)] = v
         start(result_sends(k, u, (me, me)))
-        result_local(k, u).start()
+        if k < held:
+            result_local(k, u).start()
         for c in first_sends(k, u):
             c.wait_send()
 
@@ -204,7 +216,8 @@
             c.wait_recv()
         for c in result_sends(k, u, (me, me)):
             c.wait_send()
-        result_local(k, u).wait()
+        if k < held:
+            result_local(k, u).wait()
         for c in relays(k, u, (left, right)):
             c.wait_send()
 
@@ -223,13 +236,14 @@
                 def _():
                     stage(k, u)
 
-    span = max(units, tiles - 3)
-    plan = [(0, span), (2, span + 1), (4, span + 2), (6, span + 3)]
-    plan_end = [(0, units), (2, units), (4, units), (6, units)]
-
     load_x(0).start()
     prefetch(0, 0)
     prefetch(0, 1)
+    barrier = pltpu.get_barrier_semaphore()
+    for nb in (left, right):
+        pl.semaphore_signal(barrier, inc=1, device_id={"tp": nb}, device_id_type=MESH)
+    pl.semaphore_wait(barrier, 2)
+
     for k, m in enumerate(sizes):
         load_x(k).wait()
 
@@ -259,15 +273,38 @@
 
         @pl.loop(0, units)
         def _(u, k=k):
-            prefetch(k, tiles + u + 2)
+            prefetch(k, tiles + u + 2, tiles)
             if k:
                 ticks(k - 1, tiles + u, plan)
+            if k == last:
+                ticks(k, u, end)
             wait(load_d(k, u))
             unit(k, u)
 
-    @pl.loop(0, units + 6)
+    @pl.loop(units, max(a + b for a, b in end))
     def _(q):
-        ticks(last, q, plan_end)
+        ticks(last, q, end)
+
+
+def join(cuts, a_ref, b_ref, y_ref, buf, isem, osem, bsem):
+    n, m = a_ref.shape[0], b_ref.shape[0]
+    loads, stores, rest = [], [], []
+    for i in range(cuts):
+        r = pl.ds(i * (n // cuts), n // cuts)
+        loads.append(pltpu.make_async_copy(a_ref.at[r], buf.at[r], isem.at[i]))
+        stores.append(pltpu.make_async_copy(buf.at[r], y_ref.at[r], osem.at[i]))
+        p = m // cuts
+        rest.append(pltpu.make_async_copy(
+            b_ref.at[pl.ds(i * p, p)], y_ref.at[pl.ds(n + i * p, p)], bsem.at[i]))
+    for c in loads:
+        c.start()
+    for c in rest:
+        c.start()
+    for c, o in zip(loads, stores):
+        c.wait()
+        o.start()
+    for c in stores + rest:
+        c.wait()
 
 
 def solution(mesh):
@@ -281,11 +318,12 @@
         half = top // 2
         hbm = [pltpu.with_memory_space_constraint(a, pltpu.HBM) for a in (x, w_gate, w_up, w_down)]
         bf = jnp.bfloat16
-        return pl.pallas_call(
+        split = sum(sizes[:-HELD])
+        part, kept = pl.pallas_call(
             functools.partial(kernel, n, sizes),
-            out_shape=jax.ShapeDtypeStruct((t, d), bf),
+            out_shape=(jax.ShapeDtypeStruct((split, d), bf), pltpu.VMEM((t - split, d), bf)),
             in_specs=[pl.BlockSpec(memory_space=pltpu.HBM)] * 4,
-            out_specs=pl.BlockSpec(memory_space=pltpu.HBM),
+            out_specs=(pl.BlockSpec(memory_space=pltpu.HBM), pl.BlockSpec(memory_space=pltpu.VMEM)),
             scratch_shapes=[
                 pltpu.VMEM((top, d), bf),
                 pltpu.VMEM((WBUF, max(d, f), 4 * LANES), bf),
@@ -303,9 +341,21 @@
             ],
             name="mlp",
             compiler_params=pltpu.CompilerParams(
-                collective_id=0, has_side_effects=True, vmem_limit_bytes=67043328),
+                collective_id=0, has_side_effects=True, vmem_limit_bytes=VMEM - (t - split) * d * 2),
             cost_estimate=pl.CostEstimate(flops=6 * t * d * f, bytes_accessed=6 * d * f, transcendentals=t * f),
         )(*hbm)
+        cuts = 4
+        part = pltpu.with_memory_space_constraint(part, pltpu.HBM)
+        kept = pltpu.with_memory_space_constraint(kept, pltpu.VMEM)
+        return pl.pallas_call(
+            functools.partial(join, cuts),
+            out_shape=jax.ShapeDtypeStruct((t, d), bf),
+            in_specs=[pl.BlockSpec(memory_space=pltpu.HBM), pl.BlockSpec(memory_space=pltpu.VMEM)],
+            out_specs=pl.BlockSpec(memory_space=pltpu.HBM),
+            scratch_shapes=[pltpu.VMEM((split, d), bf)] + [pltpu.SemaphoreType.DMA((cuts,))] * 3,
+            name="join",
+            compiler_params=pltpu.CompilerParams(vmem_limit_bytes=split * d * 2 + (4 << 20)),
+        )(part, kept)
 
     return jax.shard_map(
         step,

time: 543 us -> 517 us (0.952)
  local copies, waits for them, and re-layouts: 19.3 us -> 0 us
  Pallas kernels: 524 us -> 517 us
    unnamed x1 -> x0, local copies, waits for them, and re-layouts: 19.3 us -> none
    pallas_call x1 -> x2, Pallas kernels: 524 us -> 517 us  [the longest x1 505 us: step(): pl.pallas_call(functools.partial(kernel, n, sizes), out_shape=(jax.ShapeD...]
where the time goes in v2:
time: 517 us
  Pallas kernels  517 us (100%)
    pallas_call x1, Pallas kernels, step(): pl.pallas_call(functools.partial(kernel, n, sizes), out_shape=(jax.ShapeD...  505 us
    pallas_call x1, Pallas kernels, step(): pl.pallas_call(functools.partial(join, cuts), out_shape=jax.ShapeDtypeStr...  11.8 us

profile of v2, /device:TPU:112, one launch (start us, length us, event | category | flops | bytes accessed | tf_op | source)
XLA Modules:
  0.0 517.0 jit_solution(1965931536533321641)
XLA Ops:
  0.0 505.0 %mlp.1 = (bf16[704,6656]{1,0:T(8,128)(2,1)}, bf16[1344,6656]{1,0:T(8,128)(2,1)S(1)}) custom-call(bf16[2048,6656]{1,0:T(8,128)(2,1)} %x_ref.1, bf16[6656,4480]{1,0:T(8,128)(2,1)} %wg_ref.1, bf16[6656,4480]{1,0:T(8,128)(2,1)} %wu_ref.1, bf16[4480,6656]{1,0:T(8,128)(2,1)} %wd_ref.1), custom_call_target="tpu_custom_call" | custom-call | flops 366414397440 | bytes 178913280 | tf_op jit(solution)/shard_map/mlp/pallas_call | solution.py:322
  505.0 11.8 %join.1 = bf16[2048,6656]{1,0:T(8,128)(2,1)} custom-call(bf16[704,6656]{1,0:T(8,128)(2,1)} %get-tuple-element.7.a_ref, bf16[1344,6656]{1,0:T(8,128)(2,1)S(1)} %get-tuple-element.8.b_ref), custom_call_target="tpu_custom_call" | custom-call | tf_op jit(solution)/shard_map/join/pallas_call | solution.py:350
